TPU v7x, 32 devices: a whole 2x2x4 slice. The times are simulated.
32 devices in a mesh: blk: 4 (over y, x), half: 2 (over core), rep: 4 (over z).
Axes of the slice: x: 2, y: 2, z: 4, core: 2. Of those that a mesh axis runs over, the one named last changes fastest.
Arguments:
- tokens: bfloat16 [1024, 2048], P('blk'), may hold values from -6 to 6
- experts: int32 [1024, 6], P('blk'), may hold values from 0 to 63, all different within a row; in each aligned block of 256 rows (0 to 255, 256 to 511, ...) at most 32 rows name the same one
- gates: bfloat16 [1024, 6], P('blk'), may hold values from 0.099609375 to 1
- w_gate: bfloat16 [64, 1408, 2048], P('blk', ('half', 'rep')), may hold values from -0.125 to 0.125
- w_up: bfloat16 [64, 1408, 2048], P('blk', ('half', 'rep')), may hold values from -0.125 to 0.125
- w_down: bfloat16 [64, 1408, 2048], P('blk', ('half', 'rep')), may hold values from -0.15625 to 0.15625
- shared_gate: bfloat16 [1408, 2048], P(('half', 'rep')), may hold values from -0.125 to 0.125
- shared_up: bfloat16 [1408, 2048], P(('half', 'rep')), may hold values from -0.125 to 0.125
- shared_down: bfloat16 [1408, 2048], P(('half', 'rep')), may hold values from -0.15625 to 0.15625
Outputs:
- mixed: bfloat16 [1024, 2048], P('blk', ('half', 'rep'))
Inputs may be any that keep to these rules, and one draw needn't show every extreme that they name: Each row names 6 different experts. Among the 256 rows held by one index of blk no expert is named by more than 32 rows, a bound that some block reaches.
All inputs are finite; a program needn't handle non-finite values.
Results may differ from a plain program's by a relative error of at most 0.0055.
Values may be sent and summed in bfloat16 or wider, within the bound.
A program may use at most 128 MiB of HBM per device.

v0:
```python
import jax
import jax.numpy as jnp
from jax import lax
from jax.sharding import PartitionSpec as P

E = 64
CAP = 32


def hidden_units(token_rows, gate_matrix, up_weight):
    gate_values = jnp.einsum(
        "kan,ktn->kat", token_rows, gate_matrix, preferred_element_type=jnp.float32
    )
    raised_rows = jnp.einsum(
        "kan,ktn->kat", token_rows, up_weight, preferred_element_type=jnp.float32
    )
    return (jax.nn.silu(gate_values) * raised_rows).astype(jnp.bfloat16)


def place_slots(flat, ranks, block_size, which, slot_count):
    inside = ranks // block_size == which
    local = jnp.where(inside, flat * block_size + ranks % block_size, -1)
    return local[:, None] == jnp.arange(slot_count, dtype=jnp.int32)[None, :]


def per_device(tokens, experts, gates, w_gate, w_up, w_down, shared_gate, shared_up, shared_down):
    token_count = tokens.shape[0]
    width = tokens.shape[1]
    topk = experts.shape[1]
    exp_local = w_gate.shape[0]
    blk_count = lax.axis_size("blk")
    slot_block = CAP // lax.axis_size("rep")
    member_rep = lax.axis_index("rep")
    flat = experts.reshape(-1)
    onehot = (flat[:, None] == jnp.arange(E, dtype=jnp.int32)[None, :]).astype(jnp.int32)
    before = jnp.cumsum(onehot, axis=0) - onehot
    ranks = jnp.sum(before * onehot, axis=1)
    placing = place_slots(flat, ranks, slot_block, member_rep, E * slot_block).reshape(
        token_count, topk, -1
    )
    weighting = jnp.sum(
        placing.astype(jnp.float32) * gates.astype(jnp.float32)[:, :, None], axis=1
    ).astype(jnp.bfloat16)
    selector = jnp.any(placing, axis=1).astype(jnp.bfloat16)
    filled = jnp.einsum("ts,td->sd", selector, tokens, preferred_element_type=jnp.float32).astype(
        jnp.bfloat16
    )
    filled = filled.reshape(E, 1, slot_block, width)
    arrived = lax.all_to_all(filled, "blk", split_axis=0, concat_axis=1, tiled=True)
    token_rows = arrived.reshape(exp_local, -1, width)
    every_hidden = hidden_units(lax.all_gather(token_rows, "rep", axis=1, tiled=True), w_gate, w_up)
    mine = lax.all_to_all(every_hidden, "rep", split_axis=1, concat_axis=2, tiled=True)
    partial_value = jnp.einsum(
        "otv,ovj->otj",
        mine,
        lax.all_gather(w_down, "rep", axis=1, tiled=True),
        preferred_element_type=jnp.float32,
    )
    block_out = partial_value.astype(jnp.bfloat16).reshape(exp_local, blk_count, slot_block, width)
    returned = lax.all_to_all(block_out, "blk", split_axis=1, concat_axis=0, tiled=True)
    returned = returned.reshape(E * slot_block, width)
    routed = jnp.dot(weighting, returned, preferred_element_type=jnp.float32)
    shared_hidden = (
        jax.nn.silu(
            jnp.einsum("td,sd->ts", tokens, shared_gate, preferred_element_type=jnp.float32)
        )
        * jnp.einsum("td,sd->ts", tokens, shared_up, preferred_element_type=jnp.float32)
    ).astype(jnp.bfloat16)
    shared_output = jnp.dot(shared_hidden, shared_down, preferred_element_type=jnp.float32)
    routed_share = lax.psum_scatter(routed, ("half", "rep"), scatter_dimension=1, tiled=True)
    shared_share = lax.psum_scatter(shared_output, ("half", "rep"), scatter_dimension=1, tiled=True)
    total = routed_share + shared_share
    return total.astype(jnp.bfloat16)


def solution(mesh):
    return jax.shard_map(
        per_device,
        mesh=mesh,
        in_specs=(
            P("blk", None),
            P("blk", None),
            P("blk", None),
            P("blk", ("half", "rep"), None),
            P("blk", ("half", "rep"), None),
            P("blk", ("half", "rep"), None),
            P(("half", "rep"), None),
            P(("half", "rep"), None),
            P(("half", "rep"), None),
        ),
        out_specs=P("blk", ("half", "rep")),
        check_vma=False,
    )
```

profile of v0, /device:TPU:0, one launch (start us, length us, event | category | flops | bytes accessed | tf_op | source)
XLA Modules:
  0.0 1109.0 jit_solution(772665334566259263)
XLA Ops:
  6.5 0.9 copy.61
  7.8 18.1 %reduce-window.6 = s32[64,12,128]{2,1,0:T(8,128)S(1)} reduce-window(s32[64,12,128]{2,1,0:T(8,128)S(1)} %fusion.6, s32[]{:T(128)} %constant.39.clone.1), window={size=1x1x128 pad=0_0x0_0x127_0}, to_apply=%region_0.0 | reduce-window | flops 12484608 | bytes 786436 | tf_op jit(solution)/shard_map/reduce-window
  27.6 0.8 fusion.1
  28.4 30.4 %all_to_all.48 = bf16[64,1,8,2048]{3,2,1,0:T(8,128)(2,1)S(1)} all-to-all(bf16[64,1,8,2048]{3,2,1,0:T(8,128)(2,1)S(1)} %fusion.1), channel_id=1, replica_groups=mesh['blk'=4,'half'=2,'rep'=4] {'blk'}, dimensions={0} | all-to-all | bytes 4194304 | tf_op jit(solution)/shard_map/all_to_all | solution.py:49
  58.8 1.4 copy.79
  60.3 0.7 all-gather.5.cloned.1.call-update
  61.0 148.7 %all-gather.3.cloned.1.call-done = bf16[16,128,2048]{2,1,0:T(8,128)(2,1)} async-done(((bf16[16,32,2048]{2,1,0:T(8,128)(2,1)}), bf16[16,128,2048]{2,1,0:T(8,128)(2,1)}) %all-gather.3.cloned.1.call-update) | async-done | bytes 8388624 | tf_op jit(solution)/shard_map/all_gather | solution.py:51
  209.7 10.2 fusion.23
  219.9 15.1 %fusion.3 = bf16[16,128,176]{1,2,0:T(8,128)(2,1)S(1)} fusion(bf16[16,128,2048]{2,1,0:T(8,128)(2,1)} %all-gather.3.cloned.1.call-done, bf16[16,176,2048]{2,1,0:T(8,128)(2,1)} %param.13, f32[16,128,176]{1,2,0:T(8,128)S(1)} %fusion.23), kind=kOutput, calls=%fused_computation.10 | convolution fusion | flops 1478557696 | bytes 22085632 | tf_op jit(solution)/shard_map/kan,ktn->kat/dot_general | solution.py:14
  235.0 0.9 copy.71
  235.9 65.1 %all_to_all.49 = bf16[16,128,176]{2,0,1:T(8,128)(2,1)S(1)} all-to-all(bf16[16,128,176]{2,0,1:T(8,128)(2,1)S(1)} %copy.71), channel_id=1, replica_groups=mesh['blk'=4,'half'=2,'rep'=4] {'rep'}, dimensions={1} | all-to-all | bytes 1441792 | tf_op jit(solution)/shard_map/all_to_all | solution.py:52
  301.0 0.8 copy.73
  301.8 1.8 all_to_all.41
  303.6 696.8 %all-gather.5.cloned.1.call-done = bf16[16,704,2048]{2,1,0:T(8,128)(2,1)} async-done(((bf16[16,176,2048]{2,1,0:T(8,128)(2,1)}), bf16[16,704,2048]{2,1,0:T(8,128)(2,1)}) %all-gather.5.cloned.1.call-update) | async-done | bytes 46137360 | tf_op jit(solution)/shard_map/all_gather | solution.py:56
  1000.4 18.6 %fusion.2 = bf16[16,4,8,2048]{3,2,1,0:T(8,128)(2,1)S(1)} fusion(bf16[16,32,704]{2,1,0:T(8,128)(2,1)} %all_to_all.41, bf16[16,704,2048]{2,1,0:T(8,128)(2,1)} %all-gather.5.cloned.1.call-done), kind=kOutput, calls=%fused_computation.6 | convolution fusion | flops 1477443584 | bytes 48955392 | tf_op jit(solution)/shard_map/otv,ovj->otj/dot_general | solution.py:53
  1019.1 1.4 copy.74
  1020.5 4.6 all-to-all-start.2
  1025.2 0.6 select_reduce_fusion
  1025.8 1.2 fusion.24
  1027.0 2.9 fusion.5
  1029.8 20.3 %all-to-all-done.2 = bf16[16,4,8,2048]{3,2,0,1:T(8,128)(2,1)} async-done(((bf16[16,4,8,2048]{3,2,0,1:T(8,128)(2,1)}), bf16[16,4,8,2048]{3,2,0,1:T(8,128)(2,1)}, u32[]{:S(2)}, u32[]{:S(2)}) %all-to-all-start.2) | async-done | bytes 2097184 | tf_op jit(solution)/shard_map/all_to_all | solution.py:60
  1050.1 3.6 convolution_add_fusion
  1053.8 47.1 %reduce-scatter.2.cloned.1.call-done = f32[256,256]{1,0:T(8,128)} async-done(((f32[256,2048]{1,0:T(8,128)}), f32[256,256]{1,0:T(8,128)}) %reduce-scatter.2.cloned.1.call-update) | async-done | bytes 262160 | tf_op jit(solution)/shard_map/reduce_scatter | solution.py:70
  1100.9 1.6 convert_element_type.38
  (27 shorter events, 2.1 us)
Async XLA Ops:
  6.5 21.1 %copy-start = (bf16[256,2048]{1,0:T(8,128)(2,1)S(1)}, bf16[256,2048]{1,0:T(8,128)(2,1)}, u32[]{:S(2)}) copy-start(bf16[256,2048]{1,0:T(8,128)(2,1)} %param.9) | copy-start | bytes 3145732
  6.5 20.6 %copy-start.2 = (s32[256,6]{0,1:T(8,128)S(1)}, s32[256,6]{0,1:T(8,128)}, u32[]{:S(2)}) copy-start(s32[256,6]{0,1:T(8,128)} %param.10) | copy-start | bytes 18436
  6.5 203.2 %all-gather.3.cloned.1.call-start = ((), (), s32[]{:S(2)}) async-start(), calls=%async_computation.4 | async-start | bytes 10485760 | tf_op jit(solution)/shard_map/all_gather | solution.py:51
  60.2 940.2 %all-gather.5.cloned.1.call-start = ((), (), s32[]{:S(2)}) async-start(), calls=%async_computation.5 | async-start | bytes 57671680 | tf_op jit(solution)/shard_map/all_gather | solution.py:56
  1020.5 4.6 copy-start.3
  1020.5 5.3 copy-start.1
  1020.5 29.6 %all-to-all-start.2 = ((bf16[16,4,8,2048]{3,2,0,1:T(8,128)(2,1)}), bf16[16,4,8,2048]{3,2,0,1:T(8,128)(2,1)}, u32[]{:S(2)}, u32[]{:S(2)}) async-start(bf16[16,4,8,2048]{3,2,0,1:T(8,128)(2,1)} %copy.74), calls=%async_computation.2 | async-start | bytes 4194304 | tf_op jit(solution)/shard_map/all_to_all | solution.py:60
  1025.1 75.7 %reduce-scatter.2.cloned.1.call-start = ((), (), s32[]{:S(2)}) async-start(), calls=%async_computation.6 | async-start | bytes 2359296 | tf_op jit(solution)/shard_map/reduce_scatter | solution.py:70
Sparse Core Ops, SparseCore 0:
  60.4 149.3 all-gather.2
  211.3 789.0 all-gather.4
  1053.9 46.9 reduce-scatter.1
where the time goes:
time: 1110 us
  waiting for transfers between devices  914 us (82%)
  blocking collectives  95.5 us (9%)
  matrix products  52.3 us (5%)
  other arithmetic  21.3 us (2%)
  between operations  13.3 us (1%)
    all_gather x1, waiting for transfers between devices, per_device(): lax.all_gather(w_down, 'rep', axis=1, tiled=True)  697 us
    all_gather x1, waiting for transfers between devices, per_device(): lax.all_gather(token_rows, 'rep', axis=1, tiled=True)  149 us
    all_to_all x1, blocking collectives, per_device(): lax.all_to_all(every_hidden, 'rep', split_axis=1, concat_axis=2, tiled=True)  65.1 us
    reduce_scatter x1, waiting for transfers between devices, per_device(): lax.psum_scatter(routed, ('half', 'rep'), scatter_dimension=1, tiled=True)  47.1 us
    all_to_all x1, blocking collectives, per_device(): lax.all_to_all(filled, 'blk', split_axis=0, concat_axis=1, tiled=True)  30.4 us
  transfers between devices with their start and end apart: 4, of which 4 were waited for; matrix products, arithmetic and copies ran while one was open for 3% of the time, Pallas kernels for 0%

commit v1 on v0

--- a/solution.py
+++ b/solution.py
@@ -1,6 +1,10 @@
+import functools
+
 import jax
 import jax.numpy as jnp
 from jax import lax
+from jax.experimental import pallas as pl
+from jax.experimental.pallas import tpu as pltpu
 from jax.sharding import PartitionSpec as P
 
 E = 64
@@ -73,9 +77,309 @@
     return total.astype(jnp.bfloat16)
 
 
+BF = jnp.bfloat16
+F32 = jnp.float32
+NT = (((1,), (1,)), ((), ()))
+
+
+def dot(a, b):
+    return jnp.dot(a, b, preferred_element_type=F32)
+
+
+def silu_mul(g, u):
+    return (g / (1.0 + jnp.exp(-g)) * u).astype(BF)
+
+
+def fused_kernel(
+    tok, meta, sg, su, sd, wg, wu, wd, out,
+    tokb, metab, xs, hb, hs, comb, yb, gbuf, ubuf, dbuf,
+    acc, keep, dsend, drecv, asend, arecv, bsend, brecv, zsend, zrecv,
+    gsem, usem, dsem, t_s, t_r, p_s, p_r, m_s, m_r, d_s, d_r, a_s, a_r, b_s, b_r, z_s, z_r,
+):
+    T, D = tok.shape
+    el, F, _ = wg.shape
+    ring = gbuf.shape[0]
+    W = out.shape[1]
+    reps = D // (2 * W)
+    H = T // 2
+    G = t_s.shape[1]
+    R = H // G
+    me = lax.axis_index("blk")
+    c = lax.axis_index("half")
+    z = lax.axis_index("rep")
+    x = me % 2
+    y = me // 2
+    xn = y * 2 + (1 - x)
+    yn = (1 - y) * 2 + x
+    dg = (1 - y) * 2 + (1 - x)
+    n1 = (1 - c) * xn + c * yn
+    n2 = c * xn + (1 - c) * yn
+    mesh_id = pl.DeviceIdType.MESH
+
+    def weights(e, slot):
+        return (
+            pltpu.make_async_copy(wg.at[e], gbuf.at[slot], gsem.at[slot]),
+            pltpu.make_async_copy(wu.at[e], ubuf.at[slot], usem.at[slot]),
+        )
+
+    def to(src, dst, s, r, **where):
+        return pltpu.make_async_remote_copy(
+            src_ref=src, dst_ref=dst, send_sem=s, recv_sem=r, device_id=where, device_id_type=mesh_id
+        )
+
+    barrier = pltpu.get_barrier_semaphore()
+    peers = [dict(blk=n1), dict(blk=n2), dict(blk=dg), dict(half=1 - c)]
+    peers += [dict(rep=(z + k) % reps) for k in range(1, reps)]
+    for where in peers:
+        pl.semaphore_signal(barrier, inc=1, device_id=where, device_id_type=mesh_id)
+    pl.semaphore_wait(barrier, len(peers))
+
+    def rows(g):
+        return pl.ds(pl.multiple_of(c * H + g * R, R), R)
+
+    s1 = [to(tok.at[rows(g)], tokb.at[0, rows(g)], t_s.at[0, g], t_r.at[0, g], blk=n1) for g in range(G)]
+    s2 = [to(tok.at[rows(g)], tokb.at[1, rows(g)], t_s.at[1, g], t_r.at[1, g], blk=n2) for g in range(G)]
+    s3 = [to(tokb.at[0, rows(g)], tokb.at[2, rows(g)], t_s.at[2, g], t_r.at[2, g], blk=n2) for g in range(G)]
+    swap = (1, 0, 2)
+    hand = [
+        [to(tokb.at[k, rows(g)], tokb.at[swap[k], rows(g)], p_s.at[k, g], p_r.at[swap[k], g], half=1 - c) for g in range(G)]
+        for k in range(3)
+    ]
+
+    def other_rows(g):
+        return pl.ds(pl.multiple_of((1 - c) * H + g * R, R), R)
+
+    got = [
+        [to(tokb.at[swap[k], rows(g)], tokb.at[k, other_rows(g)], p_s.at[swap[k], g], p_r.at[k, g], half=1 - c) for g in range(G)]
+        for k in range(3)
+    ]
+    metas = [
+        to(meta, metab.at[k], m_s.at[k], m_r.at[k], blk=b) for k, b in enumerate((n1, n2, dg))
+    ]
+    for m in metas:
+        m.start()
+    for g in range(G):
+        s1[g].start()
+        s2[g].start()
+    for e in range(ring):
+        for w in weights(e, e):
+            w.start()
+    down_copy = pltpu.make_async_copy(wd, dbuf, dsem)
+    down_copy.start()
+
+    hs[...] = silu_mul(
+        lax.dot_general(tok[...], sg[...], NT, preferred_element_type=F32),
+        lax.dot_general(tok[...], su[...], NT, preferred_element_type=F32),
+    )
+
+    ids = (me * el + lax.broadcasted_iota(jnp.int32, (el, T), 0)).astype(F32)
+    before = (
+        lax.broadcasted_iota(jnp.int32, (T, T), 0) < lax.broadcasted_iota(jnp.int32, (T, T), 1)
+    ).astype(F32).astype(BF)
+    S = el * CAP
+    spread = (
+        lax.broadcasted_iota(jnp.int32, (S, el), 0) // CAP == lax.broadcasted_iota(jnp.int32, (S, el), 1)
+    ).astype(F32).astype(BF)
+    place = (lax.broadcasted_iota(jnp.int32, (S, T), 0) % CAP + 1).astype(F32)
+    topk = meta.shape[0] // 2
+
+    def dispatch(r, meta_ref, tok_ref):
+        named = jnp.zeros((el, T), F32)
+        gate = jnp.zeros((el, T), F32)
+        for j in range(topk):
+            hit = (meta_ref[j:j + 1, :] == ids).astype(F32)
+            named = named + hit
+            gate = gate + hit * meta_ref[topk + j:topk + j + 1, :]
+        rank = dot(named.astype(BF), before)
+        slot = dot(spread, (named * (rank + 1.0)).astype(BF))
+        chosen = (slot == place).astype(F32)
+        weight = chosen * dot(spread, gate.astype(BF))
+        comb[r] = weight.T.astype(BF)
+        pick = chosen.astype(BF)
+        step = 512
+
+        def body(k, _):
+            cols = pl.ds(pl.multiple_of(k * step, step), step)
+            part = dot(pick, tok_ref[:, cols]).astype(BF)
+            for e in range(el):
+                xs[e, r * CAP:(r + 1) * CAP, cols] = part[e * CAP:(e + 1) * CAP]
+            return 0
+
+        lax.fori_loop(0, D // step, body, 0)
+
+    dispatch(0, meta, tok)
+    for g in range(G):
+        s1[g].wait_recv()
+        s3[g].start()
+        hand[0][g].start()
+        s2[g].wait_recv()
+        hand[1][g].start()
+    for k in (0, 1):
+        metas[k].wait_recv()
+        for g in range(G):
+            got[k][g].wait_recv()
+        dispatch(k + 1, metab.at[k], tokb.at[k])
+    for g in range(G):
+        s3[g].wait_recv()
+        hand[2][g].start()
+    metas[2].wait_recv()
+    for g in range(G):
+        got[2][g].wait_recv()
+    dispatch(3, metab.at[2], tokb.at[2])
+
+    def hidden(e, slot):
+        for w in weights(e, slot):
+            w.wait()
+        rows_e = xs[e]
+        hb[e] = silu_mul(
+            lax.dot_general(rows_e, gbuf[slot], NT, preferred_element_type=F32),
+            lax.dot_general(rows_e, ubuf[slot], NT, preferred_element_type=F32),
+        )
+
+    def first(e, _):
+        hidden(e, e)
+        for w in weights(e + ring, e):
+            w.start()
+        return 0
+
+    def second(e, _):
+        hidden(e + ring, e)
+        return 0
+
+    lax.fori_loop(0, ring, first, 0)
+    lax.fori_loop(0, ring, second, 0)
+    down_copy.wait()
+
+    def partials(offset):
+        cols = pl.ds(pl.multiple_of(offset, W), W)
+
+        def body(e, _):
+            part = dot(hb[e], dbuf[e, :, cols]).astype(BF)
+            at = pl.ds(pl.multiple_of(e * CAP, CAP), CAP)
+            for r in range(4):
+                yb[r, at, :] = part[r * CAP:(r + 1) * CAP]
+            return 0
+
+        lax.fori_loop(0, el, body, 0)
+        sums = [dot(comb[r], yb[r]) for r in range(4)]
+        sums[0] = sums[0] + dot(hs[...], sd[:, cols])
+        return sums
+
+    order = (0, 2, 1, 3)
+    pending = []
+
+    def run(copy):
+        copy.start()
+        pending.append(copy)
+        return copy
+
+    dcopy, acopy, bcopy, zcopy = {}, {}, {}, {}
+
+    def chunk(i):
+        return (z + 1 + i) % reps
+
+    def stage_a(i):
+        sums = partials(((1 - c) * reps + chunk(i)) * W)
+        for r in range(4):
+            dsend[i, r] = sums[r].astype(BF)
+        dcopy[i] = run(to(dsend.at[i], drecv.at[i], d_s.at[i], d_r.at[i], half=1 - c))
+
+    def stage_b(i):
+        sums = partials((c * reps + chunk(i)) * W)
+        for r in range(4):
+            acc[r] = sums[r]
+        dcopy[i].wait_recv()
+        total = lambda r: acc[r] + drecv[i, order[r]].astype(F32)
+        asend[i, 0] = total(1).astype(BF)
+        asend[i, 1] = total(3).astype(BF)
+        acopy[i] = run(to(asend.at[i], arecv.at[i], a_s.at[i], a_r.at[i], blk=n1))
+        keep[i, 0] = total(0)
+        keep[i, 1] = total(2)
+
+    def stage_c(i):
+        acopy[i].wait_recv()
+        bsend[i] = (keep[i, 1] + arecv[i, 1].astype(F32)).astype(BF)
+        bcopy[i] = run(to(bsend.at[i], brecv.at[i], b_s.at[i], b_r.at[i], blk=n2))
+        keep[i, 0] = keep[i, 0] + arecv[i, 0].astype(F32)
+
+    def stage_d(i):
+        bcopy[i].wait_recv()
+        whole = keep[i, 0] + brecv[i].astype(F32)
+        if i < reps - 1:
+            zsend[i] = whole.astype(BF)
+            zcopy[i] = run(to(zsend.at[i], zrecv.at[i], z_s.at[i], z_r.at[i], rep=chunk(i)))
+        else:
+            for k in range(reps - 1):
+                zcopy[k].wait_recv()
+                whole = whole + zrecv[k].astype(F32)
+            out[...] = whole.astype(out.dtype)
+
+    for i in range(reps):
+        stage_a(i)
+        if i >= 1:
+            stage_c(i - 1)
+        stage_b(i)
+        if i >= 1:
+            stage_d(i - 1)
+    stage_c(reps - 1)
+    stage_d(reps - 1)
+    for copy in pending + metas + s1 + s2 + s3 + hand[0] + hand[1] + hand[2]:
+        copy.wait_send()
+
+
+def fused(tokens, experts, gates, w_gate, w_up, w_down, shared_gate, shared_up, shared_down):
+    T, D = tokens.shape
+    el, F, _ = w_gate.shape
+    reps = lax.axis_size("rep")
+    W = D // (2 * reps)
+    G = 2
+    ring = el // 2
+    meta = jnp.concatenate([experts.T.astype(F32), gates.T.astype(F32)], axis=0)
+    vm = pl.BlockSpec(memory_space=pltpu.VMEM)
+    hbm = pl.BlockSpec(memory_space=pl.ANY)
+    dma = pltpu.SemaphoreType.DMA
+    return pl.pallas_call(
+        fused_kernel,
+        out_shape=jax.ShapeDtypeStruct((T, W), BF),
+        in_specs=[vm] * 5 + [hbm] * 3,
+        out_specs=vm,
+        scratch_shapes=[
+            pltpu.VMEM((3, T, D), BF),
+            pltpu.VMEM((3,) + meta.shape, F32),
+            pltpu.VMEM((el, 4 * CAP, D), BF),
+            pltpu.VMEM((el, 4 * CAP, F), BF),
+            pltpu.VMEM((T, F), BF),
+            pltpu.VMEM((4, T, el * CAP), BF),
+            pltpu.VMEM((4, el * CAP, W), BF),
+            pltpu.VMEM((ring, F, D), BF),
+            pltpu.VMEM((ring, F, D), BF),
+            pltpu.VMEM((el, F, D), BF),
+            pltpu.VMEM((4, T, W), F32),
+            pltpu.VMEM((reps, 2, T, W), F32),
+            pltpu.VMEM((reps, 4, T, W), BF),
+            pltpu.VMEM((reps, 4, T, W), BF),
+            pltpu.VMEM((reps, 2, T, W), BF),
+            pltpu.VMEM((reps, 2, T, W), BF),
+            pltpu.VMEM((reps, T, W), BF),
+            pltpu.VMEM((reps, T, W), BF),
+            pltpu.VMEM((reps - 1, T, W), BF),
+            pltpu.VMEM((reps - 1, T, W), BF),
+            dma((ring,)), dma((ring,)), dma,
+            dma((3, G)), dma((3, G)), dma((3, G)), dma((3, G)),
+            dma((3,)), dma((3,)),
+            dma((reps,)), dma((reps,)), dma((reps,)), dma((reps,)), dma((reps,)), dma((reps,)),
+            dma((reps - 1,)), dma((reps - 1,)),
+        ],
+        compiler_params=pltpu.CompilerParams(
+            collective_id=0, has_side_effects=True, vmem_limit_bytes=64 * 1024 * 1024 - 65536
+        ),
+    )(tokens, meta, shared_gate, shared_up, shared_down, w_gate, w_up, w_down)
+
+
 def solution(mesh):
+    small = mesh.shape["blk"] == 4 and mesh.shape["half"] == 2
     return jax.shard_map(
-        per_device,
+        fused if small else per_device,
         mesh=mesh,
         in_specs=(
             P("blk", None),

time: 1110 us -> 87.5 us (0.08)
  waiting for transfers between devices: 914 us -> 0 us
  blocking collectives: 95.5 us -> 0 us
  Pallas kernels: 0 us -> 83.7 us
  matrix products: 52.3 us -> 0 us
  other arithmetic: 21.3 us -> 2 us
  between operations: 13.3 us -> 0.01 us
    all_gather x2 -> x0, waiting for transfers between devices: 846 us -> none  [the longest x1 697 us: per_device(): lax.all_gather(w_down, 'rep', axis=1, tiled=True)]
    all_to_all x2 -> x0, blocking collectives: 95.5 us -> none  [the longest x1 65.1 us: per_device(): lax.all_to_all(every_hidden, 'rep', split_axis=1, concat_axis=2, tiled=True)]
    pallas_call x0 -> x1, Pallas kernels: none -> 83.7 us  [fused(): pl.pallas_call(fused_kernel, out_shape=jax.ShapeDtypeStruct((T, W), BF),...]
    dot_general x7 -> x0, matrix products: 52.3 us -> none  [the longest x1 18.6 us: per_device(): jnp.einsum('otv,ovj->otj', mine, lax.all_gather(w_down, 'rep', axis=1, ti...]
    reduce_scatter x1 -> x0, waiting for transfers between devices: 47.1 us -> none  [per_device(): lax.psum_scatter(routed, ('half', 'rep'), scatter_dimension=1, tiled=True)]
    all_to_all x1 -> x0, waiting for transfers between devices: 20.3 us -> none  [per_device(): lax.all_to_all(block_out, 'blk', split_axis=1, concat_axis=0, tiled=True)]
    another operation x3 -> x0, other arithmetic: 18.4 us -> none
  transfers between devices with their start and end apart: 4 -> 0, of which waited for: 4 -> 0; matrix products, arithmetic and copies ran while one was open for 3% -> 0% of each run, Pallas kernels for 0% -> 0%
where the time goes in v1:
time: 87.5 us; the launch traced here: 87.2 us
  Pallas kernels  83.7 us (96%)
  other arithmetic  2 us (2%)
  local copies, waits for them, and re-layouts  1.57 us (2%)
    pallas_call x1, Pallas kernels, fused(): pl.pallas_call(fused_kernel, out_shape=jax.ShapeDtypeStruct((T, W), BF),...  83.7 us

profile of v1, /device:TPU:0, one launch (start us, length us, event | category | flops | bytes accessed | tf_op | source)
XLA Modules:
  0.0 87.2 jit_solution(3410751817573878907)
XLA Ops:
  0.0 0.7 convert_bitcast_fusion.1
  0.7 0.7 convert_bitcast_fusion
  1.4 0.6 pad_maximum_fusion.meta
  2.0 83.7 %shard_map.91 = bf16[256,256]{1,0:T(8,128)(2,1)} custom-call(bf16[256,2048]{1,0:T(8,128)(2,1)} %tok.1, f32[12,256]{1,0:T(8,128)} %pad_maximum_fusion.meta, bf16[176,2048]{1,0:T(8,128)(2,1)} %sg.1, bf16[176,2048]{1,0:T(8,128)(2,1)} %su.1, bf16[176,2048]{1,0:T(8,128)(2,1)} %sd.1, bf16[16,176,2048]{2,1,0:T(8,128)(2,1)} %wg.1, bf16[16,176,2048]{2,1,0:T(8,128)(2,1)} %wu.1, ...), custom_call_target="tpu_custom_call" | custom-call | tf_op jit(solution)/shard_map/pallas_call | solution.py:341
  85.7 1.6 %copy.11 = bf16[256,256]{1,0:T(8,128)(2,1)} copy(bf16[256,256]{1,0:T(8,128)(2,1)} %shard_map.91) | data formatting | bytes 262144

commit v2 on v1

--- a/solution.py
+++ b/solution.py
@@ -134,23 +134,28 @@
         pl.semaphore_signal(barrier, inc=1, device_id=where, device_id_type=mesh_id)
     pl.semaphore_wait(barrier, len(peers))
 
+    p = z % 2
+    zp = z + 1 - 2 * p
+
+    def piece(core, g):
+        first = (p, 2, 3, 1 - p)[g]
+        return pl.ds(pl.multiple_of(core * H + first * R, R), R)
+
     def rows(g):
-        return pl.ds(pl.multiple_of(c * H + g * R, R), R)
-
-    s1 = [to(tok.at[rows(g)], tokb.at[0, rows(g)], t_s.at[0, g], t_r.at[0, g], blk=n1) for g in range(G)]
-    s2 = [to(tok.at[rows(g)], tokb.at[1, rows(g)], t_s.at[1, g], t_r.at[1, g], blk=n2) for g in range(G)]
-    s3 = [to(tokb.at[0, rows(g)], tokb.at[2, rows(g)], t_s.at[2, g], t_r.at[2, g], blk=n2) for g in range(G)]
+        return piece(c, g)
+
+    N = G - 1
+    s1 = [to(tok.at[rows(g)], tokb.at[0, rows(g)], t_s.at[0, g], t_r.at[0, g], blk=n1) for g in range(N)]
+    s2 = [to(tok.at[rows(g)], tokb.at[1, rows(g)], t_s.at[1, g], t_r.at[1, g], blk=n2) for g in range(N)]
+    s3 = [to(tokb.at[0, rows(g)], tokb.at[2, rows(g)], t_s.at[2, g], t_r.at[2, g], blk=n2) for g in range(N)]
+    sz = [to(tokb.at[k, rows(0)], tokb.at[k, rows(0)], t_s.at[k, N], t_r.at[k, N], rep=zp) for k in range(3)]
     swap = (1, 0, 2)
     hand = [
         [to(tokb.at[k, rows(g)], tokb.at[swap[k], rows(g)], p_s.at[k, g], p_r.at[swap[k], g], half=1 - c) for g in range(G)]
         for k in range(3)
     ]
-
-    def other_rows(g):
-        return pl.ds(pl.multiple_of((1 - c) * H + g * R, R), R)
-
     got = [
-        [to(tokb.at[swap[k], rows(g)], tokb.at[k, other_rows(g)], p_s.at[swap[k], g], p_r.at[k, g], half=1 - c) for g in range(G)]
+        [to(tokb.at[swap[k], piece(1 - c, g)], tokb.at[k, piece(1 - c, g)], p_s.at[swap[k], g], p_r.at[k, g], half=1 - c) for g in range(G)]
         for k in range(3)
     ]
     metas = [
@@ -158,7 +163,7 @@
     ]
     for m in metas:
         m.start()
-    for g in range(G):
+    for g in range(N):
         s1[g].start()
         s2[g].start()
     for e in range(ring):
@@ -208,20 +213,32 @@
         lax.fori_loop(0, D // step, body, 0)
 
     dispatch(0, meta, tok)
-    for g in range(G):
+    for g in range(N):
         s1[g].wait_recv()
         s3[g].start()
+        if g == 0:
+            sz[0].start()
         hand[0][g].start()
         s2[g].wait_recv()
+        if g == 0:
+            sz[1].start()
         hand[1][g].start()
+    for k in (0, 1):
+        sz[k].wait_recv()
+        hand[k][N].start()
+    s3[0].wait_recv()
+    sz[2].start()
+    hand[2][0].start()
     for k in (0, 1):
         metas[k].wait_recv()
         for g in range(G):
             got[k][g].wait_recv()
         dispatch(k + 1, metab.at[k], tokb.at[k])
-    for g in range(G):
+    for g in range(1, N):
         s3[g].wait_recv()
         hand[2][g].start()
+    sz[2].wait_recv()
+    hand[2][N].start()
     metas[2].wait_recv()
     for g in range(G):
         got[2][g].wait_recv()
@@ -290,21 +307,21 @@
             acc[r] = sums[r]
         dcopy[i].wait_recv()
         total = lambda r: acc[r] + drecv[i, order[r]].astype(F32)
-        asend[i, 0] = total(1).astype(BF)
-        asend[i, 1] = total(3).astype(BF)
-        acopy[i] = run(to(asend.at[i], arecv.at[i], a_s.at[i], a_r.at[i], blk=n1))
+        for k, r in ((1, 3), (0, 1)):
+            asend[i, k] = total(r).astype(BF)
+            acopy[i, k] = run(to(asend.at[i, k], arecv.at[i, k], a_s.at[i, k], a_r.at[i, k], blk=n1))
         keep[i, 0] = total(0)
         keep[i, 1] = total(2)
 
     def stage_c(i):
-        acopy[i].wait_recv()
+        acopy[i, 1].wait_recv()
         bsend[i] = (keep[i, 1] + arecv[i, 1].astype(F32)).astype(BF)
         bcopy[i] = run(to(bsend.at[i], brecv.at[i], b_s.at[i], b_r.at[i], blk=n2))
-        keep[i, 0] = keep[i, 0] + arecv[i, 0].astype(F32)
 
     def stage_d(i):
+        acopy[i, 0].wait_recv()
         bcopy[i].wait_recv()
-        whole = keep[i, 0] + brecv[i].astype(F32)
+        whole = keep[i, 0] + arecv[i, 0].astype(F32) + brecv[i].astype(F32)
         if i < reps - 1:
             zsend[i] = whole.astype(BF)
             zcopy[i] = run(to(zsend.at[i], zrecv.at[i], z_s.at[i], z_r.at[i], rep=chunk(i)))
@@ -314,16 +331,19 @@
                 whole = whole + zrecv[k].astype(F32)
             out[...] = whole.astype(out.dtype)
 
-    for i in range(reps):
-        stage_a(i)
-        if i >= 1:
+    stage_a(0)
+    for i in range(reps + 2):
+        if i + 1 < reps:
+            stage_a(i + 1)
+        if i < reps:
+            stage_b(i)
+        if i == reps:
+            stage_d(i - 2)
+        if 0 <= i - 1 < reps:
             stage_c(i - 1)
-        stage_b(i)
-        if i >= 1:
-            stage_d(i - 1)
-    stage_c(reps - 1)
-    stage_d(reps - 1)
-    for copy in pending + metas + s1 + s2 + s3 + hand[0] + hand[1] + hand[2]:
+        if 0 <= i - 2 < reps and i != reps:
+            stage_d(i - 2)
+    for copy in pending + metas + s1 + s2 + s3 + sz + hand[0] + hand[1] + hand[2]:
         copy.wait_send()
 
 
@@ -332,7 +352,7 @@
     el, F, _ = w_gate.shape
     reps = lax.axis_size("rep")
     W = D // (2 * reps)
-    G = 2
+    G = 4
     ring = el // 2
     meta = jnp.concatenate([experts.T.astype(F32), gates.T.astype(F32)], axis=0)
     vm = pl.BlockSpec(memory_space=pltpu.VMEM)
@@ -367,7 +387,7 @@
             dma((ring,)), dma((ring,)), dma,
             dma((3, G)), dma((3, G)), dma((3, G)), dma((3, G)),
             dma((3,)), dma((3,)),
-            dma((reps,)), dma((reps,)), dma((reps,)), dma((reps,)), dma((reps,)), dma((reps,)),
+            dma((reps,)), dma((reps,)), dma((reps, 2)), dma((reps, 2)), dma((reps,)), dma((reps,)),
             dma((reps - 1,)), dma((reps - 1,)),
         ],
         compiler_params=pltpu.CompilerParams(
@@ -377,7 +397,7 @@
 
 
 def solution(mesh):
-    small = mesh.shape["blk"] == 4 and mesh.shape["half"] == 2
+    small = mesh.shape["blk"] == 4 and mesh.shape["half"] == 2 and mesh.shape["rep"] % 2 == 0
     return jax.shard_map(
         fused if small else per_device,
         mesh=mesh,

time: 87.5 us -> 79.4 us (0.907)
  Pallas kernels: 83.7 us -> 75.5 us
    pallas_call x1, Pallas kernels: 83.7 us -> 75.5 us  [fused(): pl.pallas_call(fused_kernel, out_shape=jax.ShapeDtypeStruct((T, W), BF),...]
where the time goes in v2:
time: 79.4 us; the launch traced here: 79.1 us
  Pallas kernels  75.5 us (95%)
  other arithmetic  2 us (3%)
  local copies, waits for them, and re-layouts  1.57 us (2%)
    pallas_call x1, Pallas kernels, fused(): pl.pallas_call(fused_kernel, out_shape=jax.ShapeDtypeStruct((T, W), BF),...  75.5 us

profile of v2, /device:TPU:0, one launch (start us, length us, event | category | flops | bytes accessed | tf_op | source)
XLA Modules:
  0.0 79.1 jit_solution(6391070192178439871)
XLA Ops:
  0.0 0.7 convert_bitcast_fusion.1
  0.7 0.7 convert_bitcast_fusion
  1.4 0.6 pad_maximum_fusion.meta
  2.0 75.5 %shard_map.91 = bf16[256,256]{1,0:T(8,128)(2,1)} custom-call(bf16[256,2048]{1,0:T(8,128)(2,1)} %tok.1, f32[12,256]{1,0:T(8,128)} %pad_maximum_fusion.meta, bf16[176,2048]{1,0:T(8,128)(2,1)} %sg.1, bf16[176,2048]{1,0:T(8,128)(2,1)} %su.1, bf16[176,2048]{1,0:T(8,128)(2,1)} %sd.1, bf16[16,176,2048]{2,1,0:T(8,128)(2,1)} %wg.1, bf16[16,176,2048]{2,1,0:T(8,128)(2,1)} %wu.1, ...), custom_call_target="tpu_custom_call" | custom-call | tf_op jit(solution)/shard_map/pallas_call | solution.py:361
  77.6 1.6 %copy.11 = bf16[256,256]{1,0:T(8,128)(2,1)} copy(bf16[256,256]{1,0:T(8,128)(2,1)} %shard_map.91) | data formatting | bytes 262144

commit v3 on v2

--- a/solution.py
+++ b/solution.py
@@ -210,7 +210,7 @@
                 xs[e, r * CAP:(r + 1) * CAP, cols] = part[e * CAP:(e + 1) * CAP]
             return 0
 
-        lax.fori_loop(0, D // step, body, 0)
+        lax.fori_loop(0, D // step, body, 0, unroll=1)
 
     dispatch(0, meta, tok)
     for g in range(N):
@@ -263,8 +263,8 @@
         hidden(e + ring, e)
         return 0
 
-    lax.fori_loop(0, ring, first, 0)
-    lax.fori_loop(0, ring, second, 0)
+    lax.fori_loop(0, ring, first, 0, unroll=4)
+    lax.fori_loop(0, ring, second, 0, unroll=4)
     down_copy.wait()
 
     def partials(offset):
@@ -277,7 +277,7 @@
                 yb[r, at, :] = part[r * CAP:(r + 1) * CAP]
             return 0
 
-        lax.fori_loop(0, el, body, 0)
+        lax.fori_loop(0, el, body, 0, unroll=8)
         sums = [dot(comb[r], yb[r]) for r in range(4)]
         sums[0] = sums[0] + dot(hs[...], sd[:, cols])
         return sums

time: 79.4 us -> 67.5 us (0.85)
  Pallas kernels: 75.5 us -> 63.7 us
    pallas_call x1, Pallas kernels: 75.5 us -> 63.7 us  [fused(): pl.pallas_call(fused_kernel, out_shape=jax.ShapeDtypeStruct((T, W), BF),...]
where the time goes in v3:
time: 67.5 us; the launch traced here: 67.3 us
  Pallas kernels  63.7 us (94%)
  other arithmetic  2 us (3%)
  local copies, waits for them, and re-layouts  1.57 us (2%)
    pallas_call x1, Pallas kernels, fused(): pl.pallas_call(fused_kernel, out_shape=jax.ShapeDtypeStruct((T, W), BF),...  63.7 us
    unnamed x1, local copies, waits for them, and re-layouts  1.57 us
    convert_element_type x2, other arithmetic, fused(): meta = jnp.concatenate([experts.T.astype(F32), gates.T.astype(F32)], axis=0)  1.39 us

profile of v3, /device:TPU:0, one launch (start us, length us, event | category | flops | bytes accessed | tf_op | source)
XLA Modules:
  0.0 67.3 jit_solution(13519353232230809647)
XLA Ops:
  0.0 0.7 %convert_bitcast_fusion.1 = f32[6,256]{1,0:T(8,128)S(1)} fusion(s32[256,6]{0,1:T(8,128)} %param.10), kind=kLoop, calls=%fused_computation.2 | loop fusion | flops 1536 | bytes 12288 | tf_op jit(solution)/shard_map/convert_element_type | solution.py:357
  0.7 0.7 %convert_bitcast_fusion = f32[6,256]{1,0:T(8,128)S(1)} fusion(bf16[256,6]{0,1:T(8,128)(2,1)} %param.11), kind=kLoop, calls=%fused_computation.1 | loop fusion | flops 1536 | bytes 9216 | tf_op jit(solution)/shard_map/convert_element_type | solution.py:357
  1.4 0.6 pad_maximum_fusion.meta
  2.0 63.7 %shard_map.91 = bf16[256,256]{1,0:T(8,128)(2,1)} custom-call(bf16[256,2048]{1,0:T(8,128)(2,1)} %tok.1, f32[12,256]{1,0:T(8,128)} %pad_maximum_fusion.meta, bf16[176,2048]{1,0:T(8,128)(2,1)} %sg.1, bf16[176,2048]{1,0:T(8,128)(2,1)} %su.1, bf16[176,2048]{1,0:T(8,128)(2,1)} %sd.1, bf16[16,176,2048]{2,1,0:T(8,128)(2,1)} %wg.1, bf16[16,176,2048]{2,1,0:T(8,128)(2,1)} %wu.1, ...), custom_call_target="tpu_custom_call" | custom-call | tf_op jit(solution)/shard_map/pallas_call | solution.py:361
  65.7 1.6 %copy.11 = bf16[256,256]{1,0:T(8,128)(2,1)} copy(bf16[256,256]{1,0:T(8,128)(2,1)} %shard_map.91) | data formatting | bytes 262144
